TPU v7x, 32 devices: a whole 2x2x4 slice. The times are simulated.
32 devices in a mesh: gx: 4 (over y, x), gy: 4 (over z), gz: 2 (over core).
Axes of the slice: x: 2, y: 2, z: 4, core: 2. Of those that a mesh axis runs over, the one named last changes fastest.
Arguments:
- fields: bfloat16 [4096, 2048], P(('gx', 'gy', 'gz')), may hold values from -6 to 6
- coordinates: float32 [3, 524288], P(None, ('gx', 'gy', 'gz')), may hold values from -1 to 1
- element_rank: int32 [524288, 1], P(('gx', 'gy', 'gz')), may hold values from 0 to 31; in each aligned block of 16384 rows (0 to 16383, 16384 to 32767, ...) at most 640 rows name the same one
- element_slot: int32 [524288], P(('gx', 'gy', 'gz')), may hold values from 0 to 127
Outputs:
- samples: float32 [4, 524288], P(None, ('gx', 'gy', 'gz'))
Inputs may be any that keep to these rules, and one draw needn't show every extreme that they name: `element_rank`: among the probes of one device no rank is named by more than 640 probes, and in some devices' blocks one rank is named by exactly 640.
All inputs are finite; a program needn't handle non-finite values.
Results may differ from a plain program's by a relative error of at most 0.0024.
Values sent between devices are 32-bit elements; how exact they have to be, the bound alone decides.
No kernel may reach another device: no remote copies, remote signals or barrier semaphores. Data moves between devices by JAX's collectives and lax.ppermute only.
A program may use at most 64 MiB of HBM per device.

v0:
```python
import math
import jax
import jax.numpy as jnp
import numpy as np
from jax import lax
from jax.sharding import PartitionSpec as P

gll_points = np.array(
    [
        -1.0,
        -0.8717401485096066,
        -0.5917001814331423,
        -0.2092992179024789,
        0.2092992179024789,
        0.5917001814331423,
        0.8717401485096066,
        1.0,
    ]
)
gll_scale = np.array(
    [1.0 / np.prod([gll_points[a] - gll_points[b] for b in range(8) if b != a]) for a in range(8)]
)


def lagrange(coord):
    offsets = coord[None, :] - jnp.asarray(gll_points, coord.dtype)[:, None]
    weights = []
    for node_a in range(8):
        factor = jnp.ones_like(coord) * gll_scale[node_a]
        for node_b in range(8):
            if node_b != node_a:
                factor = factor * offsets[node_b]
        weights.append(factor)
    return jnp.stack(weights, axis=0)


def interpolate(payload, fields):
    total_rows = payload.shape[1]
    local_count = fields.shape[0]
    block_rows = math.gcd(total_rows, 2048)
    block_count = total_rows // block_rows
    element_ids = jnp.arange(local_count, dtype=jnp.int32)

    def one_block(block):
        weight_r = lagrange(block[0])
        weight_s = lagrange(block[1])
        weight_t = lagrange(block[2]).astype(jnp.bfloat16)
        slots_block = block[3].astype(jnp.int32)
        picker = (slots_block[:, None] == element_ids[None, :]).astype(jnp.bfloat16)
        gathered = jnp.dot(picker, fields, preferred_element_type=jnp.float32).astype(jnp.bfloat16)
        gathered = gathered.reshape(block_rows, 256, 8)
        along_t = jnp.einsum("nak,kn->na", gathered, weight_t, preferred_element_type=jnp.float32)
        along_t = along_t.reshape(block_rows, 4, 8, 8)
        along_s = jnp.einsum("nfij,jn->nfi", along_t, weight_s, precision=lax.Precision.HIGHEST)
        return jnp.einsum("nfi,in->fn", along_s, weight_r, precision=lax.Precision.HIGHEST)

    blocks = payload.reshape(4, block_count, block_rows).transpose(1, 0, 2)
    result = lax.map(one_block, blocks)
    return result.transpose(1, 0, 2).reshape(4, total_rows)


def local(fields, coordinates, element_rank, element_slot):
    devices = lax.axis_size(("gx", "gy", "gz"))
    probes = element_slot.shape[0]
    capacity = 5 * probes // (4 * devices)
    target = element_rank[:, 0]
    group_rows = math.gcd(probes, 512)
    group_count = probes // group_rows
    onehot = (target[:, None] == jnp.arange(devices, dtype=jnp.int32)[None, :]).astype(jnp.bfloat16)
    onehot = onehot.reshape(group_count, group_rows, devices)
    lower = jnp.arange(group_rows)
    triangle = (lower[:, None] >= lower[None, :]).astype(jnp.bfloat16)
    within = jnp.einsum("ij,bjd->bid", triangle, onehot, preferred_element_type=jnp.float32)
    totals = within[:, -1, :]
    offsets = jnp.cumsum(totals, axis=0) - totals
    counted = (within + offsets[:, None, :]) * onehot.astype(jnp.float32)
    position = (jnp.sum(counted, axis=2).reshape(probes) - 1.0).astype(jnp.int32)
    flat = target * capacity + position
    payload = jnp.concatenate([coordinates, element_slot.astype(jnp.float32)[None, :]], axis=0)
    send = jnp.zeros((4, devices * capacity), jnp.float32).at[:, flat].set(payload)
    arrived = lax.all_to_all(
        send.reshape(4, devices, capacity),
        ("gx", "gy", "gz"),
        split_axis=1,
        concat_axis=1,
        tiled=True,
    )
    width = arrived.shape[2]
    values = interpolate(arrived.reshape(4, -1), fields)
    values = values.reshape(4, devices, width)
    returned = lax.all_to_all(values, ("gx", "gy", "gz"), split_axis=1, concat_axis=1, tiled=True)
    return returned.reshape(4, devices * capacity)[:, flat]


def solution(mesh):
    placed = (
        P(("gx", "gy", "gz"), None),
        P(None, ("gx", "gy", "gz")),
        P(("gx", "gy", "gz"), None),
        P(("gx", "gy", "gz")),
    )
    return jax.shard_map(
        local, mesh=mesh, in_specs=placed, out_specs=P(None, ("gx", "gy", "gz")), check_vma=False
    )
```

profile of v0, /device:TPU:0, one launch (start us, length us, event | category | flops | bytes accessed | tf_op | source)
XLA Modules:
  0.0 265.9 jit_solution(6529468678508932925)
XLA Ops:
  0.5 1.6 reduce.11
  2.2 0.8 fusion.8
  5.1 5.1 %copy.32 = f32[16384,4]{1,0:T(8,128)} copy(f32[16384,4]{0,1:T(4,128)S(1)} %maximum_bitcast_fusion) | data formatting | bytes 524288 | tf_op jit(solution)/shard_map/concatenate | solution.py:79
  10.2 45.3 %scatter_custom_fusion = f32[4,20480]{0,1:T(8,128)} fusion(s32[16384]{0:T(1024)S(1)} %bitcast.89, f32[16384,4]{1,0:T(8,128)} %copy.32, f32[]{:T(128)} %constant.13.clone.1), kind=kCustom, calls=%fused_computation.42 | custom fusion | bytes 328192 | tf_op jit(solution)/shard_map/scatter | solution.py:80
  55.6 6.7 %copy.33 = f32[4,32,640]{2,0,1:T(4,128)} copy(f32[4,32,640]{0,2,1:T(8,128)} %bitcast.80) | data formatting | bytes 655360 | tf_op jit(solution)/shard_map/reshape | solution.py:82
  62.2 7.5 %all-to-all-start = ((f32[4,32,640]{2,0,1:T(4,128)}), f32[4,32,640]{2,0,1:T(4,128)S(1)}, u32[]{:S(2)}, u32[]{:S(2)}) async-start(f32[4,32,640]{2,0,1:T(4,128)} %copy.33), calls=%async_computation | async-start | bytes 655360 | tf_op jit(solution)/shard_map/all_to_all | solution.py:81
  69.8 11.8 %all-to-all-done = f32[4,32,640]{2,0,1:T(4,128)S(1)} async-done(((f32[4,32,640]{2,0,1:T(4,128)}), f32[4,32,640]{2,0,1:T(4,128)S(1)}, u32[]{:S(2)}, u32[]{:S(2)}) %all-to-all-start) | async-done | bytes 327712 | tf_op jit(solution)/shard_map/all_to_all | solution.py:81
  81.7 99.4 %while.13 = (s32[]{:T(128)}, f32[10,4,2048]{2,1,0:T(4,128)}, f32[10,4,2048]{2,0,1:T(8,128)S(1)}, bf16[128,2048]{1,0:T(8,128)(2,1)}, s32[]{:T(128)}, /*index=5*/f32[8]{0:T(128)S(1)}, s32[]{:T(128)}, s32[]{}, s32[]{}, s32[]{}) while((s32[]{:T(128)}, f32[10,4,2048]{2,1,0:T(4,128)}, ...), condition=%wide.region_4.5_spmd.clone.clone.clone, body=%wide.region_3.4_spmd.sunk.clone.clone.clone.sunk | while | flops 1091790848 | bytes 7209657 | solution.py:58
  82.3 7.2 %multiply_reduce_fusion.7 = f32[2048,256]{0,1:T(8,128)S(1)} fusion(f32[2048,8]{0,1:T(8,128)S(1)} %bitcast_convert_fusion.2, bf16[128,2048]{1,0:T(8,128)(2,1)} %get-tuple-element.256, s32[2048]{0:T(1024)S(1)} %bitcast.93), kind=kOutput, calls=%fused_computation.3.clone.1 | convolution fusion | flops 1090256896 | bytes 2695168 | tf_op jit(solution)/shard_map/while/body/eval_jaxpr/dot_general | solution.py:50
  89.9 0.7 multiply_reduce_fusion.8
  92.2 7.2 %multiply_reduce_fusion.7 = f32[2048,256]{0,1:T(8,128)S(1)} fusion(f32[2048,8]{0,1:T(8,128)S(1)} %bitcast_convert_fusion.2, bf16[128,2048]{1,0:T(8,128)(2,1)} %get-tuple-element.256, s32[2048]{0:T(1024)S(1)} %bitcast.93), kind=kOutput, calls=%fused_computation.3.clone.1 | convolution fusion | flops 1090256896 | bytes 2695168 | tf_op jit(solution)/shard_map/while/body/eval_jaxpr/dot_general | solution.py:50
  99.8 0.7 multiply_reduce_fusion.8
  102.2 7.2 %multiply_reduce_fusion.7 = f32[2048,256]{0,1:T(8,128)S(1)} fusion(f32[2048,8]{0,1:T(8,128)S(1)} %bitcast_convert_fusion.2, bf16[128,2048]{1,0:T(8,128)(2,1)} %get-tuple-element.256, s32[2048]{0:T(1024)S(1)} %bitcast.93), kind=kOutput, calls=%fused_computation.3.clone.1 | convolution fusion | flops 1090256896 | bytes 2695168 | tf_op jit(solution)/shard_map/while/body/eval_jaxpr/dot_general | solution.py:50
  109.7 0.7 multiply_reduce_fusion.8
  112.1 7.2 %multiply_reduce_fusion.7 = f32[2048,256]{0,1:T(8,128)S(1)} fusion(f32[2048,8]{0,1:T(8,128)S(1)} %bitcast_convert_fusion.2, bf16[128,2048]{1,0:T(8,128)(2,1)} %get-tuple-element.256, s32[2048]{0:T(1024)S(1)} %bitcast.93), kind=kOutput, calls=%fused_computation.3.clone.1 | convolution fusion | flops 1090256896 | bytes 2695168 | tf_op jit(solution)/shard_map/while/body/eval_jaxpr/dot_general | solution.py:50
  119.7 0.7 multiply_reduce_fusion.8
  122.1 7.2 %multiply_reduce_fusion.7 = f32[2048,256]{0,1:T(8,128)S(1)} fusion(f32[2048,8]{0,1:T(8,128)S(1)} %bitcast_convert_fusion.2, bf16[128,2048]{1,0:T(8,128)(2,1)} %get-tuple-element.256, s32[2048]{0:T(1024)S(1)} %bitcast.93), kind=kOutput, calls=%fused_computation.3.clone.1 | convolution fusion | flops 1090256896 | bytes 2695168 | tf_op jit(solution)/shard_map/while/body/eval_jaxpr/dot_general | solution.py:50
  129.6 0.7 multiply_reduce_fusion.8
  132.0 7.2 %multiply_reduce_fusion.7 = f32[2048,256]{0,1:T(8,128)S(1)} fusion(f32[2048,8]{0,1:T(8,128)S(1)} %bitcast_convert_fusion.2, bf16[128,2048]{1,0:T(8,128)(2,1)} %get-tuple-element.256, s32[2048]{0:T(1024)S(1)} %bitcast.93), kind=kOutput, calls=%fused_computation.3.clone.1 | convolution fusion | flops 1090256896 | bytes 2695168 | tf_op jit(solution)/shard_map/while/body/eval_jaxpr/dot_general | solution.py:50
  139.6 0.7 multiply_reduce_fusion.8
  141.9 7.2 %multiply_reduce_fusion.7 = f32[2048,256]{0,1:T(8,128)S(1)} fusion(f32[2048,8]{0,1:T(8,128)S(1)} %bitcast_convert_fusion.2, bf16[128,2048]{1,0:T(8,128)(2,1)} %get-tuple-element.256, s32[2048]{0:T(1024)S(1)} %bitcast.93), kind=kOutput, calls=%fused_computation.3.clone.1 | convolution fusion | flops 1090256896 | bytes 2695168 | tf_op jit(solution)/shard_map/while/body/eval_jaxpr/dot_general | solution.py:50
  149.5 0.7 multiply_reduce_fusion.8
  151.9 7.2 %multiply_reduce_fusion.7 = f32[2048,256]{0,1:T(8,128)S(1)} fusion(f32[2048,8]{0,1:T(8,128)S(1)} %bitcast_convert_fusion.2, bf16[128,2048]{1,0:T(8,128)(2,1)} %get-tuple-element.256, s32[2048]{0:T(1024)S(1)} %bitcast.93), kind=kOutput, calls=%fused_computation.3.clone.1 | convolution fusion | flops 1090256896 | bytes 2695168 | tf_op jit(solution)/shard_map/while/body/eval_jaxpr/dot_general | solution.py:50
  159.4 0.7 multiply_reduce_fusion.8
  161.8 7.2 %multiply_reduce_fusion.7 = f32[2048,256]{0,1:T(8,128)S(1)} fusion(f32[2048,8]{0,1:T(8,128)S(1)} %bitcast_convert_fusion.2, bf16[128,2048]{1,0:T(8,128)(2,1)} %get-tuple-element.256, s32[2048]{0:T(1024)S(1)} %bitcast.93), kind=kOutput, calls=%fused_computation.3.clone.1 | convolution fusion | flops 1090256896 | bytes 2695168 | tf_op jit(solution)/shard_map/while/body/eval_jaxpr/dot_general | solution.py:50
  169.4 0.7 multiply_reduce_fusion.8
  171.7 7.2 %multiply_reduce_fusion.7 = f32[2048,256]{0,1:T(8,128)S(1)} fusion(f32[2048,8]{0,1:T(8,128)S(1)} %bitcast_convert_fusion.2, bf16[128,2048]{1,0:T(8,128)(2,1)} %get-tuple-element.256, s32[2048]{0:T(1024)S(1)} %bitcast.93), kind=kOutput, calls=%fused_computation.3.clone.1 | convolution fusion | flops 1090256896 | bytes 2695168 | tf_op jit(solution)/shard_map/while/body/eval_jaxpr/dot_general | solution.py:50
  181.1 2.6 all-to-all-start.1
  183.8 12.0 %all-to-all-done.1 = f32[4,32,640]{2,0,1:T(4,128)S(1)} async-done(((f32[4,32,640]{2,0,1:T(4,128)}), f32[4,32,640]{2,0,1:T(4,128)S(1)}, u32[]{:S(2)}, u32[]{:S(2)}) %all-to-all-start.1) | async-done | bytes 327712 | tf_op jit(solution)/shard_map/all_to_all | solution.py:91
  195.8 5.5 %copy.38 = f32[4,32,640]{0,2,1:T(8,128)} copy(f32[4,32,640]{2,0,1:T(4,128)S(1)} %all-to-all-done.1) | data formatting | bytes 655360 | tf_op jit(solution)/shard_map/all_to_all | solution.py:91
  201.2 58.7 %gather_fusion = f32[16384,4]{1,0:T(8,128)} fusion(f32[4,20480]{0,1:T(8,128)} %bitcast.81, s32[16384]{0:T(1024)S(1)} %broadcast_clamp_fusion), kind=kCustom, calls=%fused_computation | custom fusion | bytes 589824 | tf_op jit(solution)/shard_map/gather | solution.py:92
  259.9 5.9 %copy.39 = f32[4,16384]{1,0:T(4,128)} copy(f32[4,16384]{0,1:T(8,128)} %bitcast.82) | data formatting | bytes 524288 | tf_op jit(solution)/shard_map/gather | solution.py:92
  (226 shorter events, 23.2 us)
Async XLA Ops:
  0.0 4.8 %copy-start = (s32[16384,1]{0,1:T(1,128)S(1)}, s32[16384,1]{0,1:T(1,128)}, u32[]{:S(2)}) copy-start(s32[16384,1]{0,1:T(1,128)} %param.11) | copy-start | bytes 196612
  0.0 5.0 %copy-start.2 = (s32[16384]{0:T(1024)S(1)}, s32[16384]{0:T(1024)}, u32[]{:S(2)}) copy-start(s32[16384]{0:T(1024)} %param.12) | copy-start | bytes 196612
  0.0 5.0 %copy-start.1 = (f32[3,16384]{1,0:T(4,128)S(1)}, f32[3,16384]{1,0:T(4,128)}, u32[]{:S(2)}) copy-start(f32[3,16384]{1,0:T(4,128)} %param.10) | copy-start | bytes 589828
  55.6 26.2 %copy-start.3 = (f32[8]{0:T(128)S(1)}, f32[8]{0:T(128)}, u32[]{:S(2)}) copy-start(f32[8]{0:T(128)} %constant.81) | copy-start | bytes 100
  62.2 19.4 %all-to-all-start = ((f32[4,32,640]{2,0,1:T(4,128)}), f32[4,32,640]{2,0,1:T(4,128)S(1)}, u32[]{:S(2)}, u32[]{:S(2)}) async-start(f32[4,32,640]{2,0,1:T(4,128)} %copy.33), calls=%async_computation | async-start | bytes 655360 | tf_op jit(solution)/shard_map/all_to_all | solution.py:81
  181.1 14.6 %all-to-all-start.1 = ((f32[4,32,640]{2,0,1:T(4,128)}), f32[4,32,640]{2,0,1:T(4,128)S(1)}, u32[]{:S(2)}, u32[]{:S(2)}) async-start(f32[4,32,640]{2,0,1:T(4,128)} %bitcast.14), calls=%async_computation.1 | async-start | bytes 655360 | tf_op jit(solution)/shard_map/all_to_all | solution.py:91
where the time goes:
time: 267 us; the launch traced here: 266 us
  local copies, waits for them, and re-layouts  138 us (52%)
  matrix products  72.3 us (27%)
  waiting for transfers between devices  23.8 us (9%)
  other arithmetic  20.2 us (8%)
  starting transfers between devices  10.1 us (4%)
    dot_general x10, matrix products, one_block(): jnp.dot(picker, fields, preferred_element_type=jnp.float32)  71.5 us
    gather x2, local copies, waits for them, and re-layouts, local(): return returned.reshape(4, devices * capacity)[:, flat]  64.6 us
    scatter x1, local copies, waits for them, and re-layouts, local(): jnp.zeros((4, devices * capacity), jnp.float32).at[:, flat].set(payload)  45.3 us
    all_to_all x1, waiting for transfers between devices, local(): lax.all_to_all(values, ('gx', 'gy', 'gz'), split_axis=1, concat_axis=1, t...  12 us
    all_to_all x1, waiting for transfers between devices, local(): lax.all_to_all(send.reshape(4, devices, capacity), ('gx', 'gy', 'gz'), sp...  11.8 us
    all_to_all x1, starting transfers between devices, local(): lax.all_to_all(send.reshape(4, devices, capacity), ('gx', 'gy', 'gz'), sp...  7.51 us
    dot_general x10, other arithmetic, one_block(): jnp.einsum('nfij,jn->nfi', along_t, weight_s, precision=lax.Precision.HIG...  6.96 us
    reshape x1, local copies, waits for them, and re-layouts, local(): send.reshape(4, devices, capacity)  6.68 us
  transfers between devices with their start and end apart: 2, of which 2 were waited for; matrix products, arithmetic and copies ran while one was open for 0% of the time, Pallas kernels for 0%

commit v1 on v0

--- a/solution.py
+++ b/solution.py
@@ -78,12 +78,18 @@
     flat = target * capacity + position
     payload = jnp.concatenate([coordinates, element_slot.astype(jnp.float32)[None, :]], axis=0)
     send = jnp.zeros((4, devices * capacity), jnp.float32).at[:, flat].set(payload)
-    arrived = lax.all_to_all(
-        send.reshape(4, devices, capacity),
-        ("gx", "gy", "gz"),
-        split_axis=1,
-        concat_axis=1,
-        tiled=True,
+    arrived = jnp.concatenate(
+        lax.all_to_all(
+            jnp.stack(
+                jnp.split(
+                    send.reshape(4, devices, capacity), lax.axis_size(("gx", "gy", "gz")), axis=1
+                )
+            ),
+            ("gx", "gy", "gz"),
+            0,
+            0,
+        ),
+        axis=1,
     )
     width = arrived.shape[2]
     values = interpolate(arrived.reshape(4, -1), fields)

time: 267 us -> 322 us (1.21)
  local copies, waits for them, and re-layouts: 138 us -> 192 us
    unnamed x10 -> x73, local copies, waits for them, and re-layouts: 0.59 us -> 51.8 us
    split x0 -> x2, local copies, waits for them, and re-layouts: none -> 8.58 us  [local(): jnp.split(send.reshape(4, devices, capacity), lax.axis_size(('gx', 'gy',...]
    reshape x1, local copies, waits for them, and re-layouts: 6.68 us -> 0.02 us  [local(): jnp.concatenate(lax.all_to_all(jnp.stack(jnp.split(send.reshape(4, device...]
where the time goes in v1:
time: 322 us; the launch traced here: 320 us
  local copies, waits for them, and re-layouts  192 us (60%)
  matrix products  72.3 us (22%)
  waiting for transfers between devices  23.8 us (7%)
  other arithmetic  20.2 us (6%)
  starting transfers between devices  10.1 us (3%)
    dot_general x10, matrix products, one_block(): jnp.dot(picker, fields, preferred_element_type=jnp.float32)  71.5 us
    gather x2, local copies, waits for them, and re-layouts, local(): return returned.reshape(4, devices * capacity)[:, flat]  64.7 us
    unnamed x73, local copies, waits for them, and re-layouts  51.8 us
    scatter x1, local copies, waits for them, and re-layouts, local(): jnp.zeros((4, devices * capacity), jnp.float32).at[:, flat].set(payload)  45.3 us
    all_to_all x1, waiting for transfers between devices, local(): lax.all_to_all(values, ('gx', 'gy', 'gz'), split_axis=1, concat_axis=1, t...  12 us
    all_to_all x1, waiting for transfers between devices, local(): lax.all_to_all(jnp.stack(jnp.split(send.reshape(4, devices, capacity), la...  11.8 us
    split x2, local copies, waits for them, and re-layouts, local(): jnp.split(send.reshape(4, devices, capacity), lax.axis_size(('gx', 'gy',...  8.58 us
    all_to_all x1, starting transfers between devices, local(): lax.all_to_all(jnp.stack(jnp.split(send.reshape(4, devices, capacity), la...  7.51 us
  transfers between devices with their start and end apart: 2, of which 2 were waited for; matrix products, arithmetic and copies ran while one was open for 0% of the time, Pallas kernels for 0%

profile of v1, /device:TPU:0, one launch (start us, length us, event | category | flops | bytes accessed | tf_op | source)
XLA Modules:
  0.0 319.7 jit_solution(3954633688500111641)
XLA Ops:
  0.5 1.6 reduce.11
  5.1 5.1 %copy.94 = f32[16384,4]{1,0:T(8,128)} copy(f32[16384,4]{0,1:T(4,128)S(1)} %maximum_bitcast_fusion) | data formatting | bytes 524288 | tf_op jit(solution)/shard_map/concatenate | solution.py:79
  10.2 45.3 %scatter_custom_fusion = f32[4,20480]{0,1:T(8,128)} fusion(s32[16384]{0:T(1024)S(1)} %bitcast.160, f32[16384,4]{1,0:T(8,128)} %copy.94, f32[]{:T(128)} %constant.13.clone.1), kind=kCustom, calls=%fused_computation.42 | custom fusion | bytes 328192 | tf_op jit(solution)/shard_map/scatter | solution.py:80
  55.6 4.2 %fusion.13 = (f32[4,1,640]{0,2,1:T(8,128)}, f32[4,1,640]{0,2,1:T(8,128)}, f32[4,1,640]{0,2,1:T(8,128)}, f32[4,1,640]{0,2,1:T(8,128)}, f32[4,1,640]{0,2,1:T(8,128...) fusion(f32[4,32,640]{0,2,1:T(8,128)} %bitcast.149), kind=kLoop, calls=%fused_computation.90 | loop fusion | bytes 266240 | tf_op jit(solution)/shard_map/split | solution.py:84
  59.8 4.4 %fusion.12 = (f32[4,1,640]{0,2,1:T(8,128)S(1)}, f32[4,1,640]{0,2,1:T(8,128)S(1)}, f32[4,1,640]{0,2,1:T(8,128)S(1)}, f32[4,1,640]{0,2,1:T(8,128)S(1)}, f32[4,1,64...) fusion(f32[4,32,640]{0,2,1:T(8,128)} %bitcast.150), kind=kLoop, calls=%fused_computation.89 | loop fusion | bytes 389120 | tf_op jit(solution)/shard_map/split | solution.py:84
  65.9 1.7 copy.156
  67.6 1.7 copy.157
  69.3 1.7 copy.158
  71.0 1.7 copy.159
  72.7 1.7 copy.160
  94.0 1.3 constant_dynamic-update-slice_fusion.30
  95.3 1.3 constant_dynamic-update-slice_fusion.29
  96.6 1.3 constant_dynamic-update-slice_fusion.28
  97.9 1.3 constant_dynamic-update-slice_fusion.27
  116.0 7.5 %all-to-all-start = ((f32[32,4,1,640]{3,1,2,0:T(4,128)}), f32[32,4,1,640]{3,1,2,0:T(4,128)S(1)}, u32[]{:S(2)}, u32[]{:S(2)}) async-start(f32[32,4,1,640]{3,1,2,0:T(4,128)} %constant_dynamic-update-slice_fusion), calls=%async_computation | async-start | bytes 655360 | tf_op jit(solution)/shard_map/all_to_all | solution.py:82
  123.6 11.8 %all-to-all-done = f32[32,4,1,640]{3,1,2,0:T(4,128)S(1)} async-done(((f32[32,4,1,640]{3,1,2,0:T(4,128)}), f32[32,4,1,640]{3,1,2,0:T(4,128)S(1)}, u32[]{:S(2)}, u32[]{:S(2)}) %all-to-all-start) | async-done | bytes 327712 | tf_op jit(solution)/shard_map/all_to_all | solution.py:82
  135.5 99.4 %while.13 = (s32[]{:T(128)}, f32[10,4,2048]{2,1,0:T(4,128)}, f32[10,4,2048]{2,0,1:T(8,128)S(1)}, bf16[128,2048]{1,0:T(8,128)(2,1)}, s32[]{:T(128)}, /*index=5*/f32[8]{0:T(128)S(1)}, s32[]{:T(128)}, s32[]{}, s32[]{}, s32[]{}) while((s32[]{:T(128)}, f32[10,4,2048]{2,1,0:T(4,128)}, ...), condition=%wide.region_4.5_spmd.clone.clone.clone, body=%wide.region_3.4_spmd.sunk.clone.clone.clone.sunk | while | flops 1091790848 | bytes 7209657 | solution.py:58
  136.1 7.2 %multiply_reduce_fusion.7 = f32[2048,256]{0,1:T(8,128)S(1)} fusion(f32[2048,8]{0,1:T(8,128)S(1)} %bitcast_convert_fusion.2, bf16[128,2048]{1,0:T(8,128)(2,1)} %get-tuple-element.288, s32[2048]{0:T(1024)S(1)} %bitcast.164), kind=kOutput, calls=%fused_computation.3.clone.1 | convolution fusion | flops 1090256896 | bytes 2695168 | tf_op jit(solution)/shard_map/while/body/eval_jaxpr/dot_general | solution.py:50
  146.0 7.2 %multiply_reduce_fusion.7 = f32[2048,256]{0,1:T(8,128)S(1)} fusion(f32[2048,8]{0,1:T(8,128)S(1)} %bitcast_convert_fusion.2, bf16[128,2048]{1,0:T(8,128)(2,1)} %get-tuple-element.288, s32[2048]{0:T(1024)S(1)} %bitcast.164), kind=kOutput, calls=%fused_computation.3.clone.1 | convolution fusion | flops 1090256896 | bytes 2695168 | tf_op jit(solution)/shard_map/while/body/eval_jaxpr/dot_general | solution.py:50
  156.0 7.2 %multiply_reduce_fusion.7 = f32[2048,256]{0,1:T(8,128)S(1)} fusion(f32[2048,8]{0,1:T(8,128)S(1)} %bitcast_convert_fusion.2, bf16[128,2048]{1,0:T(8,128)(2,1)} %get-tuple-element.288, s32[2048]{0:T(1024)S(1)} %bitcast.164), kind=kOutput, calls=%fused_computation.3.clone.1 | convolution fusion | flops 1090256896 | bytes 2695168 | tf_op jit(solution)/shard_map/while/body/eval_jaxpr/dot_general | solution.py:50
  165.9 7.2 %multiply_reduce_fusion.7 = f32[2048,256]{0,1:T(8,128)S(1)} fusion(f32[2048,8]{0,1:T(8,128)S(1)} %bitcast_convert_fusion.2, bf16[128,2048]{1,0:T(8,128)(2,1)} %get-tuple-element.288, s32[2048]{0:T(1024)S(1)} %bitcast.164), kind=kOutput, calls=%fused_computation.3.clone.1 | convolution fusion | flops 1090256896 | bytes 2695168 | tf_op jit(solution)/shard_map/while/body/eval_jaxpr/dot_general | solution.py:50
  175.8 7.2 %multiply_reduce_fusion.7 = f32[2048,256]{0,1:T(8,128)S(1)} fusion(f32[2048,8]{0,1:T(8,128)S(1)} %bitcast_convert_fusion.2, bf16[128,2048]{1,0:T(8,128)(2,1)} %get-tuple-element.288, s32[2048]{0:T(1024)S(1)} %bitcast.164), kind=kOutput, calls=%fused_computation.3.clone.1 | convolution fusion | flops 1090256896 | bytes 2695168 | tf_op jit(solution)/shard_map/while/body/eval_jaxpr/dot_general | solution.py:50
  185.8 7.2 %multiply_reduce_fusion.7 = f32[2048,256]{0,1:T(8,128)S(1)} fusion(f32[2048,8]{0,1:T(8,128)S(1)} %bitcast_convert_fusion.2, bf16[128,2048]{1,0:T(8,128)(2,1)} %get-tuple-element.288, s32[2048]{0:T(1024)S(1)} %bitcast.164), kind=kOutput, calls=%fused_computation.3.clone.1 | convolution fusion | flops 1090256896 | bytes 2695168 | tf_op jit(solution)/shard_map/while/body/eval_jaxpr/dot_general | solution.py:50
  195.7 7.2 %multiply_reduce_fusion.7 = f32[2048,256]{0,1:T(8,128)S(1)} fusion(f32[2048,8]{0,1:T(8,128)S(1)} %bitcast_convert_fusion.2, bf16[128,2048]{1,0:T(8,128)(2,1)} %get-tuple-element.288, s32[2048]{0:T(1024)S(1)} %bitcast.164), kind=kOutput, calls=%fused_computation.3.clone.1 | convolution fusion | flops 1090256896 | bytes 2695168 | tf_op jit(solution)/shard_map/while/body/eval_jaxpr/dot_general | solution.py:50
  205.7 7.2 %multiply_reduce_fusion.7 = f32[2048,256]{0,1:T(8,128)S(1)} fusion(f32[2048,8]{0,1:T(8,128)S(1)} %bitcast_convert_fusion.2, bf16[128,2048]{1,0:T(8,128)(2,1)} %get-tuple-element.288, s32[2048]{0:T(1024)S(1)} %bitcast.164), kind=kOutput, calls=%fused_computation.3.clone.1 | convolution fusion | flops 1090256896 | bytes 2695168 | tf_op jit(solution)/shard_map/while/body/eval_jaxpr/dot_general | solution.py:50
  215.6 7.2 %multiply_reduce_fusion.7 = f32[2048,256]{0,1:T(8,128)S(1)} fusion(f32[2048,8]{0,1:T(8,128)S(1)} %bitcast_convert_fusion.2, bf16[128,2048]{1,0:T(8,128)(2,1)} %get-tuple-element.288, s32[2048]{0:T(1024)S(1)} %bitcast.164), kind=kOutput, calls=%fused_computation.3.clone.1 | convolution fusion | flops 1090256896 | bytes 2695168 | tf_op jit(solution)/shard_map/while/body/eval_jaxpr/dot_general | solution.py:50
  225.6 7.2 %multiply_reduce_fusion.7 = f32[2048,256]{0,1:T(8,128)S(1)} fusion(f32[2048,8]{0,1:T(8,128)S(1)} %bitcast_convert_fusion.2, bf16[128,2048]{1,0:T(8,128)(2,1)} %get-tuple-element.288, s32[2048]{0:T(1024)S(1)} %bitcast.164), kind=kOutput, calls=%fused_computation.3.clone.1 | convolution fusion | flops 1090256896 | bytes 2695168 | tf_op jit(solution)/shard_map/while/body/eval_jaxpr/dot_general | solution.py:50
  234.9 2.6 all-to-all-start.1
  237.6 12.0 %all-to-all-done.1 = f32[4,32,640]{2,0,1:T(4,128)S(1)} async-done(((f32[4,32,640]{2,0,1:T(4,128)}), f32[4,32,640]{2,0,1:T(4,128)S(1)}, u32[]{:S(2)}, u32[]{:S(2)}) %all-to-all-start.1) | async-done | bytes 327712 | tf_op jit(solution)/shard_map/all_to_all | solution.py:97
  249.6 5.4 %copy.131 = f32[4,32,640]{0,2,1:T(8,128)} copy(f32[4,32,640]{2,0,1:T(4,128)S(1)} %all-to-all-done.1) | data formatting | bytes 655360 | tf_op jit(solution)/shard_map/all_to_all | solution.py:97
  255.0 58.8 %gather_fusion = f32[16384,4]{1,0:T(8,128)} fusion(f32[4,20480]{0,1:T(8,128)} %bitcast.151, s32[16384]{0:T(1024)S(1)} %broadcast_clamp_fusion), kind=kCustom, calls=%fused_computation | custom fusion | bytes 589824 | tf_op jit(solution)/shard_map/gather | solution.py:98
  313.8 5.9 %copy.132 = f32[4,16384]{1,0:T(4,128)} copy(f32[4,16384]{0,1:T(8,128)} %bitcast.152) | data formatting | bytes 524288 | tf_op jit(solution)/shard_map/gather | solution.py:98
  (291 shorter events, 68.3 us)
Async XLA Ops:
  0.0 4.8 %copy-start = (s32[16384,1]{0,1:T(1,128)S(1)}, s32[16384,1]{0,1:T(1,128)}, u32[]{:S(2)}) copy-start(s32[16384,1]{0,1:T(1,128)} %param.11) | copy-start | bytes 196612
  0.0 5.0 %copy-start.2 = (s32[16384]{0:T(1024)S(1)}, s32[16384]{0:T(1024)}, u32[]{:S(2)}) copy-start(s32[16384]{0:T(1024)} %param.12) | copy-start | bytes 196612
  0.0 5.0 %copy-start.1 = (f32[3,16384]{1,0:T(4,128)S(1)}, f32[3,16384]{1,0:T(4,128)}, u32[]{:S(2)}) copy-start(f32[3,16384]{1,0:T(4,128)} %param.10) | copy-start | bytes 589828
  64.1 71.4 %copy-start.3 = (f32[8]{0:T(128)S(1)}, f32[8]{0:T(128)}, u32[]{:S(2)}) copy-start(f32[8]{0:T(128)} %constant.176) | copy-start | bytes 100
  116.0 19.4 %all-to-all-start = ((f32[32,4,1,640]{3,1,2,0:T(4,128)}), f32[32,4,1,640]{3,1,2,0:T(4,128)S(1)}, u32[]{:S(2)}, u32[]{:S(2)}) async-start(f32[32,4,1,640]{3,1,2,0:T(4,128)} %constant_dynamic-update-slice_fusion), calls=%async_computation | async-start | bytes 655360 | tf_op jit(solution)/shard_map/all_to_all | solution.py:82
  234.9 14.6 %all-to-all-start.1 = ((f32[4,32,640]{2,0,1:T(4,128)}), f32[4,32,640]{2,0,1:T(4,128)S(1)}, u32[]{:S(2)}, u32[]{:S(2)}) async-start(f32[4,32,640]{2,0,1:T(4,128)} %bitcast.47), calls=%async_computation.1 | async-start | bytes 655360 | tf_op jit(solution)/shard_map/all_to_all | solution.py:97
